TPU v7x, 32 devices: a whole 2x2x4 slice. The times are simulated.
32 devices in a mesh: tm: 8 (over y, x, core), sr: 4 (over z).
Axes of the slice: x: 2, y: 2, z: 4, core: 2. Of those that a mesh axis runs over, the one named last changes fastest.
Arguments:
- observations: bfloat16 [1024, 65536], P(None, ('sr', 'tm')), may hold values from -6 to 6
- loadings: float32 [65536, 128], P(('sr', 'tm')), may hold values from -0.0007324219 to 0.0007324219
- noise_precision: float32 [65536], P(('sr', 'tm')), may hold values from 0.5 to 4
- transition: float32 [128, 128], replicated, may hold values from -1 to 1, as said below
- filter_cov: float32 [128, 128], replicated, may hold values from -1 to 1, as said below
- smoother_gain: float32 [128, 128], replicated, may hold values from -1 to 1, as said below
- smoothed_cov: float32 [128, 128], replicated, may hold values from -1 to 1, as said below
Outputs:
- smoothed_factors: float32 [1024, 128], P('tm')
- new_loadings: float32 [65536, 128], P(('sr', 'tm'))
- new_transition: float32 [128, 128], replicated
Inputs may be any that keep to these rules, and one draw needn't show every extreme that they name: `transition`: the spectral radius is below one. `filter_cov`: symmetric positive definite. `smoother_gain`: the spectral radius is below one. `smoothed_cov`: symmetric positive definite.
All inputs are finite; a program needn't handle non-finite values.
Results may differ from a plain program's by a relative error of at most 0.00175.
The roundings to bfloat16 on the way count: a program that leaves them out, or rounds other values in their place, can miss the bound.
Values may be sent and summed in bfloat16 or wider, within the bound.
A program may use at most 64 MiB of HBM per device.

v0:
```python
import jax
import jax.numpy as jnp
from jax import lax
from jax.sharding import PartitionSpec as P

precise = lax.Precision.HIGHEST


def carried_in(part, axis, combine, identity, reverse):
    count = lax.axis_size(axis)
    place = lax.axis_index(axis)
    ahead = count - 1 - place if reverse else place
    gathered = jax.tree.map(lambda a: lax.all_gather(a, axis), part)
    state = jax.tree.map(lambda a, e: jnp.zeros_like(a) + jnp.asarray(e, a.dtype), part, identity)

    def one(hop, state):
        source = count - 1 - hop if reverse else hop
        return combine(
            state, jax.tree.map(lambda a: lax.dynamic_index_in_dim(a, source, 0, False), gathered)
        )

    return lax.fori_loop(0, ahead, one, state)


def shifted(value, axis, steps):
    count = lax.axis_size(axis)
    leading, last = (max(0, -steps), min(count, count - steps))
    return lax.ppermute(value, axis, [(source, source + steps) for source in range(leading, last)])


def dot_high(left, right):
    return jnp.dot(left, right, precision=precise, preferred_element_type=jnp.float32)


def matrix_power(matrix, exponent):
    result = jnp.eye(matrix.shape[0], dtype=jnp.float32)
    square = matrix
    remain = exponent
    while remain > 0:
        if remain % 2 == 1:
            result = dot_high(result, square)
        remain = remain // 2
        if remain > 0:
            square = dot_high(square, square)
    return result


def block_prefix(inputs, matrix):
    length = inputs.shape[0]
    width = inputs.shape[1]
    totals = inputs
    raised = matrix
    offset = 1
    while offset < length:
        moved = jnp.concatenate(
            [jnp.zeros((offset, width), jnp.float32), totals[: length - offset]], axis=0
        )
        totals = totals + dot_high(moved, raised.T)
        offset = offset * 2
        if offset < length:
            raised = dot_high(raised, raised)
    return totals


def propagate(start, matrix, length):
    carried = dot_high(matrix, start)[None, :]
    raised = matrix
    while carried.shape[0] < length:
        carried = jnp.concatenate([carried, dot_high(carried, raised.T)], axis=0)
        raised = dot_high(raised, raised)
    return carried


def compose(earlier, later):
    return (dot_high(later[0], earlier[0]), dot_high(later[0], earlier[1]) + later[1])


def local(
    observations, loadings, noise_precision, transition, filter_cov, smoother_gain, smoothed_cov
):
    blocks = lax.axis_size("tm")
    position = lax.axis_index("tm")
    width = transition.shape[0]
    steps_dev = observations.shape[0] // blocks
    scaled = (noise_precision[:, None] * loadings).astype(jnp.bfloat16)
    window = observations
    partial_value = lax.psum_scatter(
        jnp.dot(window, scaled, preferred_element_type=jnp.float32),
        "tm",
        scatter_dimension=0,
        tiled=True,
    )
    info_part = dot_high(loadings.T, noise_precision[:, None] * loadings)
    proj = lax.psum(partial_value, "sr")
    info = lax.psum(info_part, ("tm", "sr"))
    closed = transition - dot_high(filter_cov, dot_high(info, transition))
    inputs = dot_high(proj, filter_cov.T)
    local_filter = block_prefix(inputs, closed)
    whole_filter = matrix_power(closed, steps_dev)
    identity_pair = (jnp.eye(width, dtype=jnp.float32), jnp.zeros((width,), jnp.float32))
    entering = carried_in(
        (whole_filter, local_filter[steps_dev - 1]), "tm", compose, identity_pair, False
    )[1]
    filtered = local_filter + propagate(entering, closed, steps_dev)
    coupled = dot_high(smoother_gain, transition)
    global_rows = position * steps_dev + jnp.arange(steps_dev, dtype=jnp.int32)
    final_row = (global_rows == steps_dev * blocks - 1)[:, None]
    back = jnp.where(final_row, filtered, filtered - dot_high(filtered, coupled.T))
    local_smooth = block_prefix(back[::-1], smoother_gain)[::-1]
    whole_smooth = matrix_power(smoother_gain, steps_dev)
    arriving = carried_in((whole_smooth, local_smooth[0]), "tm", compose, identity_pair, True)[1]
    smoothed = local_smooth + propagate(arriving, smoother_gain, steps_dev)[::-1]
    factors_b = smoothed.astype(jnp.bfloat16)
    prior_row = shifted(smoothed[steps_dev - 1 :], "tm", 1)
    lag_rows = jnp.concatenate([prior_row, smoothed[: steps_dev - 1]], axis=0)
    kept_rows = jnp.where(final_row, 0.0, smoothed)
    total_part = dot_high(smoothed.T, smoothed)
    previous_part = dot_high(kept_rows.T, kept_rows)
    lagged_part = dot_high(smoothed.T, lag_rows)
    total, previous, lagged = lax.psum((total_part, previous_part, lagged_part), "tm")
    length = steps_dev * blocks
    total = total + length * smoothed_cov
    previous = previous + (length - 1) * smoothed_cov
    lagged = lagged + (length - 1) * dot_high(smoothed_cov, smoother_gain.T)
    window = observations
    cross = jnp.einsum(
        "ts,tk->sk",
        window,
        lax.all_gather(factors_b, "tm", axis=0, tiled=True),
        preferred_element_type=jnp.float32,
    )
    total_factor = jnp.linalg.cholesky(total)
    new_loadings = jax.scipy.linalg.cho_solve((total_factor, True), cross.T).T
    previous_factor = jnp.linalg.cholesky(previous)
    new_transition = jax.scipy.linalg.cho_solve((previous_factor, True), lagged.T).T
    return (smoothed, new_loadings, new_transition)


def solution(mesh):
    in_specs = (P(None, ("sr", "tm")), P(("sr", "tm"), None), P(("sr", "tm")), P(), P(), P(), P())
    out_specs = (P("tm", None), P(("sr", "tm"), None), P())
    return jax.shard_map(local, mesh=mesh, in_specs=in_specs, out_specs=out_specs, check_vma=False)
```

profile of v0, /device:TPU:0, one launch (start us, length us, event | category | flops | bytes accessed | tf_op | source)
XLA Modules:
  0.0 331.9 jit_solution(2547815003200978211)
XLA Ops:
  8.1 4.4 %fusion.13 = f32[128,128]{0,1:T(8,128)} fusion(f32[2048,128]{1,0:T(8,128)} %param.13, f32[2048]{0:T(1024)} %param.14), kind=kOutput, calls=%fused_computation.18 | convolution fusion | flops 402915328 | bytes 1122304 | tf_op jit(solution)/shard_map/dot_general | solution.py:32
  12.6 5.3 %convolution_bitcast_fusion.2 = f32[1024,128]{0,1:T(8,128)} fusion(bf16[1024,2048]{1,0:T(8,128)(2,1)} %param.12, f32[2048,128]{1,0:T(8,128)} %param.13, f32[2048]{0:T(1024)} %param.14), kind=kOutput, calls=%fused_computation.15 | convolution fusion | flops 537395200 | bytes 5775360 | tf_op jit(solution)/shard_map/dot_general | solution.py:88
  20.3 11.4 %all-gather.1 = f32[1024,128]{1,0:T(8,128)S(1)} all-gather(f32[128,128]{1,0:T(8,128)S(1)} %fusion.46), channel_id=3, replica_groups=mesh['tm'=8,'sr'=4] {'tm'}, dimensions={0}, use_global_device_ids=true | all-gather | bytes 589824 | tf_op jit(solution)/shard_map/all_gather | solution.py:13
  31.7 105.7 %all-reduce.21.cloned.1.call-done = f32[128,128]{0,1:T(8,128)} async-done(((f32[128,128]{0,1:T(8,128)}), f32[128,128]{0,1:T(8,128)}) %all-reduce.21.cloned.1.call-update) | async-done | bytes 65552 | tf_op jit(solution)/shard_map/psum | solution.py:95
  137.3 1.1 fusion.125
  138.5 0.3 fusion.16
  140.6 10.4 %all-gather = f32[1024,128]{1,0:T(8,128)S(1)} all-gather(f32[128,128]{1,0:T(8,128)S(1)} %fusion.47), channel_id=2, replica_groups=mesh['tm'=8,'sr'=4] {'tm'}, dimensions={0}, use_global_device_ids=true | all-gather | bytes 589824 | tf_op jit(solution)/shard_map/all_gather | solution.py:13
  151.0 25.0 %all-reduce.19.cloned.1.call-done = f32[128,128]{0,1:T(8,128)} async-done(((f32[128,128]{0,1:T(8,128)}), f32[128,128]{0,1:T(8,128)}) %all-reduce.19.cloned.1.call-update) | async-done | bytes 65552 | tf_op jit(solution)/shard_map/psum | solution.py:94
  176.0 1.1 fusion.124
  179.0 8.8 %all-gather.2 = f32[8,1,128]{2,1,0:T(1,128)S(1)} all-gather(f32[1,1,128]{2,1,0:T(1,128)S(1)} %slice_bitcast_fusion.1), channel_id=1, replica_groups=mesh['tm'=8,'sr'=4] {'tm'}, dimensions={0}, use_global_device_ids=true | all-gather | bytes 4608 | tf_op jit(solution)/shard_map/all_gather | solution.py:13
  191.8 9.7 %all-gather.3 = f32[8,1,128]{2,1,0:T(1,128)S(1)} all-gather(f32[1,1,128]{2,1,0:T(1,128)S(1)} %slice_bitcast_fusion), channel_id=1, replica_groups=mesh['tm'=8,'sr'=4] {'tm'}, dimensions={0}, use_global_device_ids=true | all-gather | bytes 4608 | tf_op jit(solution)/shard_map/all_gather | solution.py:13
  201.5 1.6 while.27
  205.1 1.0 fusion.36
  206.1 0.9 fusion.147
  207.0 2.0 collective-permute-start
  209.0 8.7 %all_gather.27 = bf16[1024,128]{1,0:T(8,128)(2,1)S(1)} all-gather(bf16[128,128]{1,0:T(8,128)(2,1)S(1)} %get-tuple-element.157), channel_id=1, replica_groups=mesh['tm'=8,'sr'=4] {'tm'}, dimensions={0}, use_global_device_ids=true | all-gather | bytes 294912 | tf_op jit(solution)/shard_map/all_gather | solution.py:129
  217.7 0.9 fusion.21
  218.7 2.9 fusion.148
  221.6 49.8 %all-reduce.23.cloned.1.call-done = (f32[128,128]{0,1:T(8,128)}, f32[128,128]{0,1:T(8,128)}, f32[128,128]{0,1:T(8,128)}) async-done(((f32[128,128]{0,1:T(8,128)}, f32[128,128]{0,1:T(8,128)}, f32[128,128]{0,1:T(8,128)}), (f32[128,128]{0,1:T(8,128)}, f32[128,128]{0,1:T(8,128)}, f32[128,128]{0,1:T(8,128)})) %all-reduce.23.cloned.1.call-update) | async-done | bytes 196624 | tf_op jit(solution)/shard_map/psum | solution.py:120
  271.4 0.9 multiply_add_fusion
  272.5 11.7 %cholesky.55 = f32[128,128]{1,0:T(8,128)S(1)} custom-call(f32[128,128]{1,0:T(8,128)S(1)} %get-tuple-element.161), custom_call_target="Cholesky" | custom-call | tf_op jit(solution)/shard_map/jit(cholesky)/cholesky | solution.py:134
  284.3 0.6 compare_reduce_fusion
  284.9 0.7 fusion.20
  285.6 9.8 %custom-call.17 = f32[1,128,128]{1,2,0:T(8,128)S(1)} custom-call(f32[1,128,128]{2,1,0:T(8,128)S(1)} %fusion.20), custom_call_target="InvertDiagBlocksLowerTriangular" | custom-call | tf_op jit(solution)/shard_map/jit(_cho_solve)/triangular_solve | solution.py:135
  295.4 1.1 fusion.27
  296.5 0.9 fusion.25
  297.4 11.7 %cholesky.44 = f32[128,128]{1,0:T(8,128)S(1)} custom-call(f32[128,128]{1,0:T(8,128)S(1)} %get-tuple-element.162), custom_call_target="Cholesky" | custom-call | tf_op jit(solution)/shard_map/jit(cholesky)/cholesky | solution.py:132
  309.2 0.6 compare_reduce_fusion.1
  309.8 0.7 fusion.19
  310.5 9.9 %custom-call.16 = f32[1,128,128]{1,2,0:T(8,128)S(1)} custom-call(f32[1,128,128]{2,1,0:T(8,128)S(1)} %fusion.19), custom_call_target="InvertDiagBlocksLowerTriangular" | custom-call | tf_op jit(solution)/shard_map/jit(_cho_solve)/triangular_solve | solution.py:133
  320.5 1.1 fusion.32
  321.5 2.8 fusion.30
  (119 shorter events, 13.9 us)
Async XLA Ops:
  8.0 10.0 %copy-start = (f32[128,128]{1,0:T(8,128)S(1)}, f32[128,128]{1,0:T(8,128)}, u32[]{:S(2)}) copy-start(f32[128,128]{1,0:T(8,128)} %param.17) | copy-start | bytes 196612
  8.0 9.9 %copy-start.2 = (f32[128,128]{1,0:T(8,128)S(1)}, f32[128,128]{1,0:T(8,128)}, u32[]{:S(2)}) copy-start(f32[128,128]{1,0:T(8,128)} %param.15) | copy-start | bytes 196612
  8.0 10.4 %copy-start.3 = (f32[128,128]{1,0:T(8,128)S(1)}, f32[128,128]{1,0:T(8,128)}, u32[]{:S(2)}) copy-start(f32[128,128]{1,0:T(8,128)} %param.18) | copy-start | bytes 196612
  8.0 129.3 %all-reduce.21.cloned.1.call-start = ((), (), s32[]{:S(2)}) async-start(), calls=%async_computation.3 | async-start | bytes 131072 | tf_op jit(solution)/shard_map/psum | solution.py:95
  12.5 126.0 %copy-start.4 = (f32[128,128]{1,0:T(8,128)S(1)}, f32[128,128]{1,0:T(8,128)}, u32[]{:S(2)}) copy-start(f32[128,128]{1,0:T(8,128)} %param.16) | copy-start | bytes 196612
  12.5 128.0 %reduce-scatter.2.cloned.1.call-start = ((), (), s32[]{:S(2)}) async-start(), calls=%async_computation.1 | async-start | bytes 589824 | tf_op jit(solution)/shard_map/reduce_scatter | solution.py:87
  17.9 158.1 %all-reduce.19.cloned.1.call-start = ((), (), s32[]{:S(2)}) async-start(), calls=%async_computation.2 | async-start | bytes 131072 | tf_op jit(solution)/shard_map/psum | solution.py:94
  140.6 130.9 %all-reduce.23.cloned.1.call-start = ((), (), s32[]{:S(2)}) async-start(), calls=%async_computation.4 | async-start | bytes 393216 | tf_op jit(solution)/shard_map/psum | solution.py:120
  205.1 105.4 %copy-start.1 = (f32[128,128]{1,0:T(8,128)}, f32[128,128]{1,0:T(8,128)S(1)}, u32[]{:S(2)}) copy-start(f32[128,128]{1,0:T(8,128)S(1)} %get-tuple-element.158) | copy-start | bytes 196612
  207.0 10.7 %collective-permute-start = (f32[1,128]{1,0:T(1,128)S(1)}, f32[1,128]{1,0:T(1,128)S(1)}, u32[]{:S(2)}, u32[]{:S(2)}) collective-permute-start(f32[1,128]{1,0:T(1,128)S(1)} %slice.121), channel_id=1, source_target_pairs={{0,4},{4,8},{8,12},{12,16},{16,20},{20,24},{24,28},{1,5},{5,9},{9,... | collective-permute-start | bytes 1544 | tf_op jit(solution)/shard_map/ppermute | solution.py:28
Sparse Core Ops, SparseCore 0:
  15.0 122.2 all-reduce.20
Sparse Core Ops, SparseCore 1:
  18.0 36.8 reduce-scatter.1
  140.6 35.2 all-reduce.18
  218.7 52.6 all-reduce.22
where the time goes:
time: 332 us
  waiting for transfers between devices  181 us (55%)
  blocking collectives  48.9 us (15%)
  other arithmetic  46.8 us (14%)
  matrix products  36.4 us (11%)
  between operations  16.2 us (5%)
    psum x1, waiting for transfers between devices, local(): info = lax.psum(info_part, ('tm', 'sr'))  106 us
    psum x1, waiting for transfers between devices, local(): lax.psum((total_part, previous_part, lagged_part), 'tm')  49.8 us
    all_gather x4, blocking collectives, carried_in(): gathered = jax.tree.map(lambda a: lax.all_gather(a, axis), part)  40.2 us
    psum x1, waiting for transfers between devices, local(): proj = lax.psum(partial_value, 'sr')  25 us
    dot_general x63, matrix products, dot_high(): jnp.dot(left, right, precision=precise, preferred_element_type=jnp.float32)  22.3 us
    another operation x3, other arithmetic, local(): previous_factor = jnp.linalg.cholesky(previous)  12.4 us
    another operation x3, other arithmetic, local(): total_factor = jnp.linalg.cholesky(total)  12.4 us
    another operation x2, other arithmetic, local(): new_loadings = jax.scipy.linalg.cho_solve((total_factor, True), cross.T).T  10.6 us
  transfers between devices with their start and end apart: 5, of which 3 were waited for; matrix products, arithmetic and copies ran while one was open for 4% of the time, Pallas kernels for 0%

commit v1 on v0

--- a/solution.py
+++ b/solution.py
@@ -92,7 +92,7 @@
     )
     info_part = dot_high(loadings.T, noise_precision[:, None] * loadings)
     proj = lax.psum(partial_value, "sr")
-    info = lax.psum(info_part, ("tm", "sr"))
+    info = lax.psum(lax.psum(info_part, "sr"), "tm")
     closed = transition - dot_high(filter_cov, dot_high(info, transition))
     inputs = dot_high(proj, filter_cov.T)
     local_filter = block_prefix(inputs, closed)

time: 332 us -> 311 us (0.937)
  waiting for transfers between devices: 181 us -> 166 us
    psum x1, waiting for transfers between devices: 106 us -> 54.8 us  [local(): info = lax.psum(lax.psum(info_part, 'sr'), 'tm')]
    reduce_scatter x1, waiting for transfers between devices: 0.03 us -> 32 us  [local(): lax.psum_scatter(jnp.dot(window, scaled, preferred_element_type=jnp.float...]
    all_gather x4, blocking collectives: 40.2 us -> 36.7 us  [carried_in(): gathered = jax.tree.map(lambda a: lax.all_gather(a, axis), part)]
  transfers between devices with their start and end apart: 5 -> 5, of which waited for: 3 -> 4; matrix products, arithmetic and copies ran while one was open for 4% -> 3% of each run, Pallas kernels for 0% -> 0%
where the time goes in v1:
time: 311 us
  waiting for transfers between devices  166 us (53%)
  other arithmetic  46.8 us (15%)
  blocking collectives  45.8 us (15%)
  matrix products  34.9 us (11%)
  between operations  14.3 us (5%)
    psum x1, waiting for transfers between devices, local(): info = lax.psum(lax.psum(info_part, 'sr'), 'tm')  54.8 us
    psum x1, waiting for transfers between devices, local(): lax.psum((total_part, previous_part, lagged_part), 'tm')  51.6 us
    all_gather x4, blocking collectives, carried_in(): gathered = jax.tree.map(lambda a: lax.all_gather(a, axis), part)  36.7 us
    reduce_scatter x1, waiting for transfers between devices, local(): lax.psum_scatter(jnp.dot(window, scaled, preferred_element_type=jnp.float...  32 us
    psum x1, waiting for transfers between devices, local(): proj = lax.psum(partial_value, 'sr')  27.6 us
    dot_general x63, matrix products, dot_high(): jnp.dot(left, right, precision=precise, preferred_element_type=jnp.float32)  20.7 us
    another operation x3, other arithmetic, local(): previous_factor = jnp.linalg.cholesky(previous)  12.4 us
    another operation x3, other arithmetic, local(): total_factor = jnp.linalg.cholesky(total)  12.4 us
  transfers between devices with their start and end apart: 5, of which 4 were waited for; matrix products, arithmetic and copies ran while one was open for 3% of the time, Pallas kernels for 0%

profile of v1, /device:TPU:0, one launch (start us, length us, event | category | flops | bytes accessed | tf_op | source)
XLA Modules:
  0.0 310.9 jit_solution(2182300111337458826)
XLA Ops:
  7.3 5.4 %convolution_bitcast_fusion.2 = f32[1024,128]{0,1:T(8,128)} fusion(bf16[1024,2048]{1,0:T(8,128)(2,1)} %param.12, f32[2048,128]{1,0:T(8,128)} %param.13, f32[2048]{0:T(1024)} %param.14), kind=kOutput, calls=%fused_computation.15 | convolution fusion | flops 537395200 | bytes 5775360 | tf_op jit(solution)/shard_map/dot_general | solution.py:88
  14.9 2.8 fusion.13
  17.7 32.0 %reduce-scatter.2.cloned.1.call-done = f32[128,128]{0,1:T(8,128)} async-done(((f32[1024,128]{0,1:T(8,128)}), f32[128,128]{0,1:T(8,128)}) %reduce-scatter.2.cloned.1.call-update) | async-done | bytes 65552 | tf_op jit(solution)/shard_map/reduce_scatter | solution.py:87
  49.9 9.8 %all-gather.1 = f32[1024,128]{1,0:T(8,128)S(1)} all-gather(f32[128,128]{1,0:T(8,128)S(1)} %fusion.46), channel_id=3, replica_groups=mesh['tm'=8,'sr'=4] {'tm'}, dimensions={0}, use_global_device_ids=true | all-gather | bytes 589824 | tf_op jit(solution)/shard_map/all_gather | solution.py:13
  59.7 27.6 %all-reduce.24.cloned.1.call-done = (f32[128,128]{0,1:T(8,128)}, f32[128,128]{0,1:T(8,128)}) async-done(((f32[128,128]{0,1:T(8,128)}, f32[128,128]{0,1:T(8,128)}), (f32[128,128]{0,1:T(8,128)}, f32[128,128]{0,1:T(8,128)})) %all-reduce.24.cloned.1.call-update) | async-done | bytes 131088 | tf_op jit(solution)/shard_map/psum | solution.py:94
  87.4 1.1 fusion.124
  88.5 54.8 %all-reduce.20.cloned.1.call-done = f32[128,128]{0,1:T(8,128)} async-done(((f32[128,128]{0,1:T(8,128)}), f32[128,128]{0,1:T(8,128)}) %all-reduce.20.cloned.1.call-update) | async-done | bytes 65552 | tf_op jit(solution)/shard_map/psum | solution.py:95
  143.3 1.1 fusion.125
  148.2 8.1 %all-gather.2 = f32[8,1,128]{2,1,0:T(1,128)S(1)} all-gather(f32[1,1,128]{2,1,0:T(1,128)S(1)} %slice_bitcast_fusion.1), channel_id=1, replica_groups=mesh['tm'=8,'sr'=4] {'tm'}, dimensions={0}, use_global_device_ids=true | all-gather | bytes 4608 | tf_op jit(solution)/shard_map/all_gather | solution.py:13
  156.5 9.5 %all-gather = f32[1024,128]{1,0:T(8,128)S(1)} all-gather(f32[128,128]{1,0:T(8,128)S(1)} %fusion.47), channel_id=2, replica_groups=mesh['tm'=8,'sr'=4] {'tm'}, dimensions={0}, use_global_device_ids=true | all-gather | bytes 589824 | tf_op jit(solution)/shard_map/all_gather | solution.py:13
  170.2 9.2 %all-gather.3 = f32[8,1,128]{2,1,0:T(1,128)S(1)} all-gather(f32[1,1,128]{2,1,0:T(1,128)S(1)} %slice_bitcast_fusion), channel_id=1, replica_groups=mesh['tm'=8,'sr'=4] {'tm'}, dimensions={0}, use_global_device_ids=true | all-gather | bytes 4608 | tf_op jit(solution)/shard_map/all_gather | solution.py:13
  179.4 1.6 while.27
  183.0 1.0 fusion.36
  184.0 0.9 fusion.147
  184.9 2.0 collective-permute-start
  186.9 9.1 %all_gather.27 = bf16[1024,128]{1,0:T(8,128)(2,1)S(1)} all-gather(bf16[128,128]{1,0:T(8,128)(2,1)S(1)} %get-tuple-element.159), channel_id=1, replica_groups=mesh['tm'=8,'sr'=4] {'tm'}, dimensions={0}, use_global_device_ids=true | all-gather | bytes 294912 | tf_op jit(solution)/shard_map/all_gather | solution.py:129
  196.0 0.9 fusion.21
  197.0 2.9 fusion.148
  199.9 51.6 %all-reduce.22.cloned.1.call-done = (f32[128,128]{0,1:T(8,128)}, f32[128,128]{0,1:T(8,128)}, f32[128,128]{0,1:T(8,128)}) async-done(((f32[128,128]{0,1:T(8,128)}, f32[128,128]{0,1:T(8,128)}, f32[128,128]{0,1:T(8,128)}), (f32[128,128]{0,1:T(8,128)}, f32[128,128]{0,1:T(8,128)}, f32[128,128]{0,1:T(8,128)})) %all-reduce.22.cloned.1.call-update) | async-done | bytes 196624 | tf_op jit(solution)/shard_map/psum | solution.py:120
  251.5 0.9 multiply_add_fusion
  252.6 11.7 %cholesky.55 = f32[128,128]{1,0:T(8,128)S(1)} custom-call(f32[128,128]{1,0:T(8,128)S(1)} %get-tuple-element.163), custom_call_target="Cholesky" | custom-call | tf_op jit(solution)/shard_map/jit(cholesky)/cholesky | solution.py:134
  264.4 0.6 compare_reduce_fusion
  265.0 0.7 fusion.20
  265.7 9.8 %custom-call.17 = f32[1,128,128]{1,2,0:T(8,128)S(1)} custom-call(f32[1,128,128]{2,1,0:T(8,128)S(1)} %fusion.20), custom_call_target="InvertDiagBlocksLowerTriangular" | custom-call | tf_op jit(solution)/shard_map/jit(_cho_solve)/triangular_solve | solution.py:135
  275.5 1.1 fusion.27
  276.6 0.9 fusion.25
  277.5 11.7 %cholesky.44 = f32[128,128]{1,0:T(8,128)S(1)} custom-call(f32[128,128]{1,0:T(8,128)S(1)} %get-tuple-element.164), custom_call_target="Cholesky" | custom-call | tf_op jit(solution)/shard_map/jit(cholesky)/cholesky | solution.py:132
  289.3 0.6 compare_reduce_fusion.1
  289.9 0.7 fusion.19
  290.6 10.0 %custom-call.16 = f32[1,128,128]{1,2,0:T(8,128)S(1)} custom-call(f32[1,128,128]{2,1,0:T(8,128)S(1)} %fusion.19), custom_call_target="InvertDiagBlocksLowerTriangular" | custom-call | tf_op jit(solution)/shard_map/jit(_cho_solve)/triangular_solve | solution.py:133
  300.5 1.1 fusion.32
  301.6 2.8 fusion.30
  (123 shorter events, 14.1 us)
Async XLA Ops:
  7.2 5.5 %copy-start = (f32[128,128]{1,0:T(8,128)S(1)}, f32[128,128]{1,0:T(8,128)}, u32[]{:S(2)}) copy-start(f32[128,128]{1,0:T(8,128)} %param.17) | copy-start | bytes 196612
  7.2 7.7 %copy-start.6 = (f32[2048]{0:T(1024)S(1)}, f32[2048]{0:T(1024)}, u32[]{:S(2)}) copy-start(f32[2048]{0:T(1024)} %param.14) | copy-start | bytes 24580
  7.2 7.7 %copy-start.1 = (f32[2048,128]{1,0:T(8,128)S(1)}, f32[2048,128]{1,0:T(8,128)}, u32[]{:S(2)}) copy-start(f32[2048,128]{1,0:T(8,128)} %param.13) | copy-start | bytes 3145732
  7.2 7.2 %copy-start.4 = (f32[128,128]{1,0:T(8,128)S(1)}, f32[128,128]{1,0:T(8,128)}, u32[]{:S(2)}) copy-start(f32[128,128]{1,0:T(8,128)} %param.18) | copy-start | bytes 196612
  7.2 7.4 %copy-start.3 = (f32[128,128]{1,0:T(8,128)S(1)}, f32[128,128]{1,0:T(8,128)}, u32[]{:S(2)}) copy-start(f32[128,128]{1,0:T(8,128)} %param.15) | copy-start | bytes 196612
  7.2 42.4 %reduce-scatter.2.cloned.1.call-start = ((), (), s32[]{:S(2)}) async-start(), calls=%async_computation.1 | async-start | bytes 589824 | tf_op jit(solution)/shard_map/reduce_scatter | solution.py:87
  12.6 74.8 %copy-start.5 = (f32[128,128]{1,0:T(8,128)S(1)}, f32[128,128]{1,0:T(8,128)}, u32[]{:S(2)}) copy-start(f32[128,128]{1,0:T(8,128)} %param.16) | copy-start | bytes 196612
  12.7 74.7 %all-reduce.24.cloned.1.call-start = ((), (), s32[]{:S(2)}) async-start(), calls=%async_computation.4 | async-start | bytes 262144 | tf_op jit(solution)/shard_map/psum | solution.py:94
  49.7 93.7 %all-reduce.20.cloned.1.call-start = ((), (), s32[]{:S(2)}) async-start(), calls=%async_computation.2 | async-start | bytes 131072 | tf_op jit(solution)/shard_map/psum | solution.py:95
  87.3 164.2 %all-reduce.22.cloned.1.call-start = ((), (), s32[]{:S(2)}) async-start(), calls=%async_computation.3 | async-start | bytes 393216 | tf_op jit(solution)/shard_map/psum | solution.py:120
  183.0 107.6 %copy-start.2 = (f32[128,128]{1,0:T(8,128)}, f32[128,128]{1,0:T(8,128)S(1)}, u32[]{:S(2)}) copy-start(f32[128,128]{1,0:T(8,128)S(1)} %get-tuple-element.160) | copy-start | bytes 196612
  184.9 11.1 %collective-permute-start = (f32[1,128]{1,0:T(1,128)S(1)}, f32[1,128]{1,0:T(1,128)S(1)}, u32[]{:S(2)}, u32[]{:S(2)}) collective-permute-start(f32[1,128]{1,0:T(1,128)S(1)} %slice.121), channel_id=1, source_target_pairs={{0,4},{4,8},{8,12},{12,16},{16,20},{20,24},{24,28},{1,5},{5,9},{9,... | collective-permute-start | bytes 1544 | tf_op jit(solution)/shard_map/ppermute | solution.py:28
Sparse Core Ops, SparseCore 0:
  12.8 36.8 reduce-scatter.1
  52.6 34.6 all-reduce.23
  90.4 52.9 all-reduce.19
  197.1 54.3 all-reduce.21
